TPU v7x, 32 devices: a whole 2x2x4 slice. The times are simulated.
32 devices in a mesh: dp: 8 (over z, x), ctx: 2 (over core), tensor: 2 (over y).
Axes of the slice: x: 2, y: 2, z: 4, core: 2. Of those that a mesh axis runs over, the one named last changes fastest.
Arguments:
- tokens: bfloat16 [16, 736, 1152], P(('dp', 'tensor'), 'ctx'), may hold values from -6 to 6
- teacher: bfloat16 [16, 736, 1152], P(('dp', 'tensor'), 'ctx'), may hold values from -6 to 6
- valid_len: int32 [16], P(('dp', 'tensor')), may hold values from 0 to 729, as said below
- ln1_gain: bfloat16 [1152], P(('dp', 'ctx')), may hold values from 0.5 to 1.5
- ln1_bias: bfloat16 [1152], P(('dp', 'ctx')), may hold values from -4 to 4
- w_q: bfloat16 [1152, 1152], P(('dp', 'ctx'), 'tensor'), may hold values from -0.25 to 0.25
- b_q: bfloat16 [1152], P('tensor'), may hold values from -4 to 4
- w_k: bfloat16 [1152, 1152], P(('dp', 'ctx'), 'tensor'), may hold values from -0.25 to 0.25
- w_v: bfloat16 [1152, 1152], P(('dp', 'ctx'), 'tensor'), may hold values from -0.1875 to 0.1875
- b_v: bfloat16 [1152], P('tensor'), may hold values from -4 to 4
- w_o: bfloat16 [1152, 1152], P('tensor', ('dp', 'ctx')), may hold values from -1.5 to 1.5
- b_o: bfloat16 [1152], P(('dp', 'ctx')), may hold values from -6 to 6
- ln2_gain: bfloat16 [1152], P(('dp', 'ctx')), may hold values from 0.5 to 1.5
- ln2_bias: bfloat16 [1152], P(('dp', 'ctx')), may hold values from -4 to 4
- w_up: bfloat16 [1152, 4304], P(('dp', 'ctx'), 'tensor'), may hold values from -0.1875 to 0.1875
- b_up: bfloat16 [4304], P('tensor'), may hold values from -6 to 6
- w_down: bfloat16 [4304, 1152], P('tensor', ('dp', 'ctx')), may hold values from -0.09375 to 0.09375
- b_down: bfloat16 [1152], P(('dp', 'ctx')), may hold values from -6 to 6
Outputs:
- layer_out: bfloat16 [16, 736, 1152], P(('dp', 'tensor'), 'ctx')
- loss: float32 [], replicated
- tokens_grad: float32 [16, 736, 1152], P(('dp', 'tensor'), 'ctx')
- ln1_gain_grad: float32 [1152], P(('dp', 'ctx'))
- ln1_bias_grad: float32 [1152], P(('dp', 'ctx'))
- w_q_grad: float32 [1152, 1152], P(('dp', 'ctx'), 'tensor')
- b_q_grad: float32 [1152], P('tensor')
- w_k_grad: float32 [1152, 1152], P(('dp', 'ctx'), 'tensor')
- w_v_grad: float32 [1152, 1152], P(('dp', 'ctx'), 'tensor')
- b_v_grad: float32 [1152], P('tensor')
- w_o_grad: float32 [1152, 1152], P('tensor', ('dp', 'ctx'))
- b_o_grad: float32 [1152], P(('dp', 'ctx'))
- ln2_gain_grad: float32 [1152], P(('dp', 'ctx'))
- ln2_bias_grad: float32 [1152], P(('dp', 'ctx'))
- w_up_grad: float32 [1152, 4304], P(('dp', 'ctx'), 'tensor')
- b_up_grad: float32 [4304], P('tensor')
- w_down_grad: float32 [4304, 1152], P('tensor', ('dp', 'ctx'))
- b_down_grad: float32 [1152], P(('dp', 'ctx'))
Inputs may be any that keep to these rules, and one draw needn't show every extreme that they name: The first valid_len[s] token positions of slot s are valid and the others are not; the last slot has exactly 729 valid tokens.
All inputs are finite; a program needn't handle non-finite values.
Results may differ from a plain program's by a relative error of at most 0.014.
Values may be sent and summed in bfloat16 or wider, within the bound.
A program may use at most 192 MiB of HBM per device.

v0:
```python
import jax
import jax.numpy as jnp
from jax import lax
from jax.sharding import PartitionSpec as P

HD = 72
REAL = 729
EPSILON = 1e-06
GELU_C = 0.7978845608028654
GELU_K = 0.044715
BF = jnp.bfloat16
F32 = jnp.float32


def norm_forward(row_values, gain_vec, shift_vec):
    average = jnp.mean(row_values, axis=-1, keepdims=True)
    centred = row_values - average
    spread = jnp.mean(centred * centred, axis=-1, keepdims=True)
    inverse = lax.rsqrt(spread + EPSILON)
    unit_rows = centred * inverse
    return (unit_rows * gain_vec + shift_vec, unit_rows, inverse)


def norm_backward(upstream, unit_rows, inverse, gain_vec):
    scaled = upstream * gain_vec
    inner_sum = (
        scaled
        - jnp.mean(scaled, axis=-1, keepdims=True)
        - unit_rows * jnp.mean(scaled * unit_rows, axis=-1, keepdims=True)
    )
    return (inner_sum * inverse, jnp.sum(upstream * unit_rows, axis=0), jnp.sum(upstream, axis=0))


def gelu_tanh(values):
    return 0.5 * values * (1.0 + jnp.tanh(GELU_C * (values + GELU_K * values * values * values)))


def gelu_slope(values):
    tanh_part = jnp.tanh(GELU_C * (values + GELU_K * values * values * values))
    return 0.5 * (1.0 + tanh_part) + 0.5 * values * (1.0 - tanh_part * tanh_part) * GELU_C * (
        1.0 + 3.0 * GELU_K * values * values
    )


def swap(values, axis):
    return lax.ppermute(values, axis, [(0, 1), (1, 0)])


def tensor_gather(values):
    if lax.axis_size("tensor") == 2:
        return jnp.stack([values, swap(values, "tensor")])
    return lax.all_gather(values, "tensor", axis=0)


def tensor_reduce(partials):
    if lax.axis_size("tensor") == 2:
        return partials[0] + swap(partials[1].astype(BF), "tensor").astype(F32)
    return lax.psum_scatter(partials.astype(BF), "tensor", scatter_dimension=0).astype(F32)


def ctx_gather(values):
    if lax.axis_size("ctx") == 2:
        return jnp.concatenate([values, swap(values, "ctx")], axis=2)
    return lax.all_gather(values, "ctx", axis=2, tiled=True)


def ctx_reduce(values, half_len):
    if lax.axis_size("ctx") == 2:
        other = swap(values[:, :, half_len:].astype(BF), "ctx")
        return values[:, :, :half_len] + other.astype(F32)
    return lax.psum_scatter(values.astype(BF), "ctx", scatter_dimension=2, tiled=True).astype(F32)


def key_positions(half_len):
    n_ctx = lax.axis_size("ctx")
    local = jnp.arange(half_len * n_ctx)
    if n_ctx == 2:
        me = lax.axis_index("ctx")
        block = jnp.where(local < half_len, me, 1 - me)
        return block * half_len + local % half_len
    return local


def tree_sum(values, axes):
    for axis in axes:
        size = lax.axis_size(axis)
        if size & size - 1:
            values = jax.tree.map(lambda v: lax.psum(v, axis), values)
            continue
        step = 1
        while step < size:
            perm = [(i, i ^ step) for i in range(size)]
            values = jax.tree.map(lambda v: v + lax.ppermute(v, axis, perm), values)
            step *= 2
    return values


def on_device(
    tokens,
    teacher,
    valid_len,
    ln1_gain,
    ln1_bias,
    w_q,
    b_q,
    w_k,
    w_v,
    b_v,
    w_o,
    b_o,
    ln2_gain,
    ln2_bias,
    w_up,
    b_up,
    w_down,
    b_down,
):
    own_images, half_len, width = tokens.shape
    n_t = lax.axis_size("tensor")
    piece, head_width = w_q.shape
    local_heads = head_width // HD
    hidden_width = w_up.shape[1]
    rows = own_images * half_len
    images = n_t * own_images
    valid_count = tree_sum(jnp.sum(valid_len.astype(jnp.int32)), ("tensor", "dp")).astype(F32)
    valid_count, tokens = lax.optimization_barrier((valid_count, tokens))
    pad_hidden = -hidden_width % 128
    pad_out = -head_width % 128
    vector_rows = jnp.stack([ln1_gain, ln1_bias, b_o, ln2_gain, ln2_bias, b_down], axis=1)
    vector_slot = jnp.pad(vector_rows, ((0, 0), (0, head_width - vector_rows.shape[1])))
    attn_pack = jnp.stack([w_q, w_k, w_v, w_o.T, vector_slot])
    attn_full = lax.all_gather(attn_pack, ("dp", "ctx"), axis=1, tiled=True)
    mlp_pack = jnp.pad(jnp.stack([w_up, w_down.T]), ((0, 0), (0, 0), (0, pad_hidden)))
    mlp_full = lax.all_gather(mlp_pack, ("dp", "ctx"), axis=1, tiled=True)
    qkv_w = attn_full[:3].reshape(3, width, local_heads, HD)
    out_wt = attn_full[3]
    vectors = attn_full[4][:, :6].astype(F32)
    gain_one, shift_one, out_bias, gain_two, shift_two, down_bias = [
        vectors[:, i] for i in range(6)
    ]
    up_w, down_wt = (mlp_full[0], mlp_full[1])
    up_b = jnp.pad(b_up.astype(F32), (0, pad_hidden))
    out_per_head = out_wt.reshape(width, local_heads, HD)
    qkv_bias = jnp.stack([b_q.astype(F32), jnp.zeros((head_width,), F32), b_v.astype(F32)]).reshape(
        3, 1, local_heads, 1, HD
    )
    inputs = tokens.astype(F32).reshape(rows, width)
    normed, unit_one, inverse_one = norm_forward(inputs, gain_one, shift_one)
    normed_every_row = tensor_gather(normed.astype(BF)).reshape(images, half_len, width)
    qkv_rows = (
        jnp.einsum("pro,tojx->tpjrx", normed_every_row, qkv_w, preferred_element_type=F32)
        + qkv_bias
    ).astype(BF)
    queries, key_rows, value_rows = (qkv_rows[0], qkv_rows[1], qkv_rows[2])
    key_all = ctx_gather(key_rows)
    value_all = ctx_gather(value_rows)
    usable = key_positions(half_len) < REAL
    score_scale = HD ** (-0.5)
    raw_scores = jnp.einsum("bhqe,bhke->bhqk", queries, key_all, preferred_element_type=F32)
    scores = jnp.where(usable, raw_scores * score_scale, -1e30)
    summit = jnp.max(scores, axis=-1, keepdims=True)
    exp_total = jnp.sum(jnp.exp(scores - summit), axis=-1, keepdims=True)
    log_totals = summit + jnp.log(exp_total)
    soft_weights = jnp.exp(scores - log_totals).astype(BF)
    mixed_per_head = jnp.einsum(
        "bhqk,bhke->bhqe", soft_weights, value_all, preferred_element_type=F32
    ).astype(BF)
    attn_terms = jnp.einsum(
        "lscm,dsm->lcd", mixed_per_head, out_per_head, preferred_element_type=F32
    )
    attn_sum = tensor_reduce(attn_terms.reshape(n_t, rows, width))
    hidden = inputs + attn_sum + out_bias
    normed_two, unit_two, inverse_two = norm_forward(hidden, gain_two, shift_two)
    normed_two_all = tensor_gather(normed_two.astype(BF)).reshape(images * half_len, width)
    before = jnp.dot(normed_two_all, up_w, preferred_element_type=F32) + up_b
    active = gelu_tanh(before).astype(BF)
    mlp_terms = jnp.einsum("rf,df->rd", active, down_wt, preferred_element_type=F32)
    result = hidden + tensor_reduce(mlp_terms.reshape(n_t, rows, width)) + down_bias
    layer_out = result.astype(BF).reshape(own_images, half_len, width)
    position = lax.axis_index("ctx") * half_len + jnp.arange(half_len)
    valid_rows = (position[None, :] < valid_len[:, None]).astype(F32).reshape(rows)
    error_rows = result - teacher.astype(F32).reshape(rows, width)
    partial_value = 0.5 * jnp.sum(valid_rows * jnp.mean(error_rows * error_rows, axis=-1))
    slot_total = own_images * lax.axis_size("dp") * n_t
    factor = slot_total * (half_len * lax.axis_size("ctx")) / valid_count
    grad_out = error_rows * (valid_rows[:, None] * factor)
    grad_rows = tensor_gather(grad_out.astype(BF)).reshape(images * half_len, width)
    down_grad_t = jnp.einsum("rd,rf->df", grad_rows, active, preferred_element_type=F32)
    active_grad = jnp.einsum("rd,df->rf", grad_rows, down_wt, preferred_element_type=F32)
    before_grad = (active_grad * gelu_slope(before)).astype(BF)
    up_bias_grad = jnp.sum(before_grad[:, :hidden_width], axis=0, dtype=F32)
    up_grad = jnp.einsum("rd,rf->df", normed_two_all, before_grad, preferred_element_type=F32)
    mlp_grad_pack = jnp.concatenate([up_grad.astype(BF), down_grad_t.astype(BF)], axis=1)
    norm_two_terms = jnp.einsum("rf,df->rd", before_grad, up_w, preferred_element_type=F32)
    norm_two_grad = tensor_reduce(norm_two_terms.reshape(n_t, rows, width))
    hidden_back, gain_two_grad, shift_two_grad = norm_backward(
        norm_two_grad, unit_two, inverse_two, gain_two
    )
    hidden_grad = grad_out + hidden_back
    mlp_grad_pack, hidden_grad = lax.optimization_barrier((mlp_grad_pack, hidden_grad))
    mlp_grads = lax.psum_scatter(mlp_grad_pack, ("dp", "ctx"), scatter_dimension=0, tiled=True)
    down_bias_grad = jnp.sum(grad_out, axis=0)
    out_bias_grad = jnp.sum(hidden_grad, axis=0)
    hidden_token_rows = tensor_gather(hidden_grad.astype(BF)).reshape(images, half_len, width)
    out_grad_t = jnp.einsum(
        "lcd,lscm->dsm", hidden_token_rows, mixed_per_head, preferred_element_type=F32
    ).reshape(width, head_width)
    mixed_grad = jnp.einsum(
        "lcd,dsm->lscm", hidden_token_rows, out_per_head, preferred_element_type=F32
    ).astype(BF)
    soft_full = jnp.exp(scores - log_totals)
    soft_grad = jnp.einsum("bhqe,bhke->bhqk", mixed_grad, value_all, preferred_element_type=F32)
    value_grads = jnp.einsum(
        "bhqk,bhqe->bhke", soft_full.astype(BF), mixed_grad, preferred_element_type=F32
    )
    inner_sum = jnp.sum(soft_full * soft_grad, axis=-1, keepdims=True)
    score_grad = (soft_full * (soft_grad - inner_sum)).astype(BF)
    query_grads = (
        jnp.einsum("bhqk,bhke->bhqe", score_grad, key_all, preferred_element_type=F32) * score_scale
    )
    key_grads = (
        jnp.einsum("bhqk,bhqe->bhke", score_grad, queries, preferred_element_type=F32) * score_scale
    )
    key_reduced_precision = ctx_reduce(key_grads, half_len).astype(BF)
    value_reduced_precision = ctx_reduce(value_grads, half_len).astype(BF)
    query_reduced_precision = query_grads.astype(BF)
    query_bias_grad = jnp.sum(query_reduced_precision, axis=(0, 2), dtype=F32).reshape(head_width)
    value_bias_grad = jnp.sum(value_reduced_precision, axis=(0, 2), dtype=F32).reshape(head_width)
    qkv_grads = jnp.stack([query_reduced_precision, key_reduced_precision, value_reduced_precision])
    qkv_weight_grad = jnp.einsum(
        "okz,toaks->ztas", normed_every_row, qkv_grads, preferred_element_type=F32
    ).reshape(width, 3 * head_width)
    attn_grads = lax.psum_scatter(
        jnp.concatenate(
            [jnp.pad(out_grad_t.astype(BF), ((0, 0), (0, pad_out))), qkv_weight_grad.astype(BF)],
            axis=1,
        ),
        ("dp", "ctx"),
        scatter_dimension=0,
        tiled=True,
    )
    norm_one_terms = jnp.einsum("toaks,tzas->okz", qkv_grads, qkv_w, preferred_element_type=F32)
    norm_one_grad = tensor_reduce(norm_one_terms.reshape(n_t, rows, width))
    input_back, gain_one_grad, shift_one_grad = norm_backward(
        norm_one_grad, unit_one, inverse_one, gain_one
    )
    tokens_grad = (hidden_grad + input_back).reshape(own_images, half_len, width)
    row_sums = jnp.concatenate(
        [
            gain_one_grad,
            shift_one_grad,
            out_bias_grad,
            gain_two_grad,
            shift_two_grad,
            down_bias_grad,
            partial_value.reshape(1),
        ]
    )
    head_sums = jnp.concatenate([query_bias_grad, value_bias_grad, up_bias_grad])
    row_sums, head_sums = tree_sum((row_sums, head_sums), ("ctx", "dp"))
    row_sums = tree_sum(row_sums, ("tensor",))
    loss_value = row_sums[6 * width] / valid_count
    piece_start = lax.axis_index(("dp", "ctx")) * piece
    vector_shards = [
        lax.dynamic_slice_in_dim(row_sums, i * width + piece_start, piece) for i in range(6)
    ]
    query_bias_sum = head_sums[:head_width]
    value_bias_sum = head_sums[head_width : 2 * head_width]
    up_bias_sum = head_sums[2 * head_width :]
    attn_grads = attn_grads.astype(F32)
    mlp_grads = mlp_grads.astype(F32)
    out_cols = head_width + pad_out
    attn_grads = [
        attn_grads[:, out_cols + i * head_width : out_cols + (i + 1) * head_width] for i in range(3)
    ] + [attn_grads[:, :head_width]]
    hidden_cols = hidden_width + pad_hidden
    mlp_grads = [
        mlp_grads[:, :hidden_width],
        mlp_grads[:, hidden_cols : hidden_cols + hidden_width],
    ]
    return (
        layer_out,
        loss_value,
        tokens_grad,
        vector_shards[0],
        vector_shards[1],
        attn_grads[0],
        query_bias_sum,
        attn_grads[1],
        attn_grads[2],
        value_bias_sum,
        attn_grads[3].T,
        vector_shards[2],
        vector_shards[3],
        vector_shards[4],
        mlp_grads[0],
        up_bias_sum,
        mlp_grads[1].T,
        vector_shards[5],
    )


def solution(mesh):
    return jax.shard_map(
        on_device,
        mesh=mesh,
        in_specs=(
            P(("dp", "tensor"), "ctx", None),
            P(("dp", "tensor"), "ctx", None),
            P(("dp", "tensor")),
            P(("dp", "ctx")),
            P(("dp", "ctx")),
            P(("dp", "ctx"), "tensor"),
            P("tensor"),
            P(("dp", "ctx"), "tensor"),
            P(("dp", "ctx"), "tensor"),
            P("tensor"),
            P("tensor", ("dp", "ctx")),
            P(("dp", "ctx")),
            P(("dp", "ctx")),
            P(("dp", "ctx")),
            P(("dp", "ctx"), "tensor"),
            P("tensor"),
            P("tensor", ("dp", "ctx")),
            P(("dp", "ctx")),
        ),
        out_specs=(
            P(("dp", "tensor"), "ctx", None),
            P(),
            P(("dp", "tensor"), "ctx", None),
            P(("dp", "ctx")),
            P(("dp", "ctx")),
            P(("dp", "ctx"), "tensor"),
            P("tensor"),
            P(("dp", "ctx"), "tensor"),
            P(("dp", "ctx"), "tensor"),
            P("tensor"),
            P("tensor", ("dp", "ctx")),
            P(("dp", "ctx")),
            P(("dp", "ctx")),
            P(("dp", "ctx")),
            P(("dp", "ctx"), "tensor"),
            P("tensor"),
            P("tensor", ("dp", "ctx")),
            P(("dp", "ctx")),
        ),
        check_vma=False,
    )
```

profile of v0, /device:TPU:0, one launch (start us, length us, event | category | flops | bytes accessed | tf_op | source)
XLA Modules:
  0.0 603.0 jit_solution(12647250671530605282)
XLA Ops:
  34.9 49.4 %all-gather.3.cloned.1.call-done = bf16[5,1152,576]{2,1,0:T(8,128)(2,1)} async-done(((bf16[5,72,576]{2,1,0:T(8,128)(2,1)}), bf16[5,1152,576]{2,1,0:T(8,128)(2,1)}) %all-gather.3.cloned.1.call-update) | async-done | bytes 6635536 | tf_op jit(solution)/shard_map/all_gather | solution.py:132
  90.5 4.7 slice.162
  95.2 6.7 %copy.80 = bf16[3,1152,576]{1,2,0:T(8,128)(2,1)} copy(bf16[3,1152,576]{2,1,0:T(8,128)(2,1)} %slice.162) | data formatting | bytes 7962624 | tf_op jit(solution)/shard_map/slice | solution.py:135
  102.4 7.5 %collective-permute-done.4 = bf16[368,1152]{1,0:T(8,128)(2,1)} collective-permute-done((bf16[368,1152]{1,0:T(8,128)(2,1)S(1)}, bf16[368,1152]{1,0:T(8,128)(2,1)}, u32[]{:S(2)}, u32[]{:S(2)}) %collective-permute-start.4) | collective-permute-done | bytes 847904 | tf_op jit(solution)/shard_map/ppermute | solution.py:46
  109.8 6.1 %fusion.15 = bf16[3,2,8,368,72]{3,4,1,2,0:T(8,128)(2,1)S(1)} fusion(f32[3,8,72]{2,1,0:T(8,128)S(1)} %maximum_bitcast_fusion, bf16[3,1152,8,72,1]{1,3,4,2,0:T(8,128)(2,1)} %bitcast.218, bf16[1,368,1152]{2,1,0:T(8,128)(2,1)} %bitcast.18, bf16[1,368,1152]{2,1,0:T(8,128)(2,1)S(1)} %fusion.39), kind=kOutput, calls=%fused_computation.35 | convolution fusion | flops 2936180736 | bytes 8227584 | tf_op jit(solution)/shard_map/pro,tojx->tpjrx/dot_general | solution.py:151
  120.1 5.5 fusion
  125.7 4.7 exponential_reduce_fusion
  132.5 6.5 %fusion.57 = bf16[2,8,368,72]{2,3,1,0:T(8,128)(2,1)} fusion(f32[2,8,368,736]{3,2,1,0:T(8,128)S(1)} %get-tuple-element.68, f32[2,8,368]{2,1,0:T(8,128)S(1)} %log_add_fusion, pred[736]{0:T(1024)(128)(4,1)S(1)} %fusion.82, bf16[2,8,368,72]{2,3,0,1:T(8,128)(2,1)S(1)} %collective-permute-done.6, bf16[2,8,368,72]{2,3,0,1:T(8,128)(2,1)S(1)} %copy-done.15), kind=kOutput, calls=%fused_computation.116 | convolution fusion | flops 645183488 | bytes 19902176 | tf_op jit(solution)/shard_map/bhqk,bhke->bhqe/dot_general | solution.py:165
  143.6 19.4 %collective-permute-done.7 = bf16[368,1152]{1,0:T(8,128)(2,1)S(1)} collective-permute-done((bf16[368,1152]{1,0:T(8,128)(2,1)S(1)}, bf16[368,1152]{1,0:T(8,128)(2,1)S(1)}, u32[]{:S(2)}, u32[]{:S(2)}) %collective-permute-start.7) | collective-permute-done | bytes 847904 | tf_op jit(solution)/shard_map/ppermute | solution.py:46
  166.0 18.3 %collective-permute-done.8 = bf16[368,1152]{1,0:T(8,128)(2,1)S(1)} collective-permute-done((bf16[368,1152]{1,0:T(8,128)(2,1)S(1)}, bf16[368,1152]{1,0:T(8,128)(2,1)S(1)}, u32[]{:S(2)}, u32[]{:S(2)}) %collective-permute-start.8) | collective-permute-done | bytes 847904 | tf_op jit(solution)/shard_map/ppermute | solution.py:46
  185.7 7.6 %fusion.12 = f32[736,2176]{1,0:T(8,128)S(1)} fusion(bf16[736,1152]{1,0:T(8,128)(2,1)} %bitcast.222, bf16[2,1152,2176]{2,1,0:T(8,128)(2,1)} %all-gather.5.cloned.1.call-done), kind=kOutput, calls=%fused_computation.29 | convolution fusion | flops 3689938944 | bytes 13115392 | tf_op jit(solution)/shard_map/dot_general | solution.py:175
  193.3 5.8 fusion.13
  203.4 18.1 %collective-permute-done.9 = bf16[368,1152]{1,0:T(8,128)(2,1)} collective-permute-done((bf16[368,1152]{1,0:T(8,128)(2,1)}, bf16[368,1152]{1,0:T(8,128)(2,1)}, u32[]{:S(2)}, u32[]{:S(2)}) %collective-permute-start.9) | collective-permute-done | bytes 847904 | tf_op jit(solution)/shard_map/ppermute | solution.py:46
  226.6 17.0 %collective-permute-done.10 = bf16[368,1152]{1,0:T(8,128)(2,1)S(1)} collective-permute-done((bf16[368,1152]{1,0:T(8,128)(2,1)S(1)}, bf16[368,1152]{1,0:T(8,128)(2,1)S(1)}, u32[]{:S(2)}, u32[]{:S(2)}) %collective-permute-start.10) | collective-permute-done | bytes 847904 | tf_op jit(solution)/shard_map/ppermute | solution.py:46
  243.9 5.5 convolution_convert_fusion
  249.4 9.5 %fusion.9 = bf16[736,2176]{1,0:T(8,128)(2,1)S(1)} fusion(bf16[736,1152]{1,0:T(8,128)(2,1)S(1)} %bitcast.225, f32[736,2176]{1,0:T(8,128)} %copy-done.51, bf16[2,1152,2176]{2,1,0:T(8,128)(2,1)S(1)} %bitcast.240, f32[2176]{0:T(1024)S(1)} %pad_convert_fusion), kind=kOutput, calls=%fused_computation.21 | convolution fusion | flops 3721969664 | bytes 16330752 | tf_op jit(solution)/shard_map/rd,df->rf/dot_general | solution.py:189
  258.9 4.8 convolution_convert_fusion.1
  272.5 4.7 pad_maximum_fusion
  277.3 11.7 %collective-permute-done.11 = bf16[368,1152]{1,0:T(8,128)(2,1)} collective-permute-done((bf16[368,1152]{1,0:T(8,128)(2,1)}, bf16[368,1152]{1,0:T(8,128)(2,1)}, u32[]{:S(2)}, u32[]{:S(2)}) %collective-permute-start.11) | collective-permute-done | bytes 847904 | tf_op jit(solution)/shard_map/ppermute | solution.py:46
  297.3 15.2 %collective-permute-done.12 = bf16[368,1152]{1,0:T(8,128)(2,1)S(1)} collective-permute-done((bf16[368,1152]{1,0:T(8,128)(2,1)S(1)}, bf16[368,1152]{1,0:T(8,128)(2,1)S(1)}, u32[]{:S(2)}, u32[]{:S(2)}) %collective-permute-start.12) | collective-permute-done | bytes 847904 | tf_op jit(solution)/shard_map/ppermute | solution.py:46
  313.9 8.4 %fusion.73 = f32[2,8,736,72]{2,3,1,0:T(8,128)S(1)} fusion(bf16[2,8,368,72]{2,3,0,1:T(8,128)(2,1)S(1)} %fusion.65, f32[2,8,368,736]{3,2,1,0:T(8,128)} %copy-done, f32[2,8,368]{2,1,0:T(8,128)S(1)} %log_add_fusion, pred[736]{0:T(1024)(128)(4,1)S(1)} %fusion.82), kind=kOutput, calls=%fused_computation.129 | convolution fusion | flops 641368064 | bytes 21597920 | tf_op jit(solution)/shard_map/bhqk,bhqe->bhke/dot_general | solution.py:213
  325.4 14.7 %multiply_reduce_fusion = (f32[2,8,368]{2,1,0:T(8,128)S(1)}, f32[2,8,368,736]{3,2,1,0:T(8,128)}) fusion(f32[2,8,368,736]{3,2,1,0:T(8,128)} %copy-done, f32[2,8,368]{2,1,0:T(8,128)S(1)} %log_add_fusion, pred[736]{0:T(1024)(128)(4,1)S(1)} %fusion.82, bf16[2,8,368,72]{2,3,0,1:T(8,128)(2,1)S(1)} %fusion.65, bf16[2,8,368,72]{2,3,0,1:T(8,128)(2,1)S(1)} %copy-done.30, ...), kind=kOutput, calls=%fused_computation.1 | convolution fusion | flops 649087232 | bytes 37260000 | tf_op jit(solution)/shard_map/bhqe,bhke->bhqk/dot_general | solution.py:212
  340.0 12.9 %multiply_convert_fusion = bf16[2,8,368,736]{3,2,1,0:T(8,128)(2,1)S(1)} fusion(f32[2,8,368,736]{3,2,1,0:T(8,128)} %get-tuple-element.70, f32[2,8,368,736]{3,2,1,0:T(8,128)} %copy-done, f32[2,8,368]{2,1,0:T(8,128)S(1)} %get-tuple-element.69, f32[2,8,368]{2,1,0:T(8,128)S(1)} %log_add_fusion, pred[736]{0:T(1024)(128)(4,1)S(1)} %fusion.82), kind=kLoop, calls=%fused_computation | loop fusion | flops 26001408 | bytes 43383520 | tf_op jit(solution)/shard_map/convert_element_type | solution.py:217
  364.0 7.5 %convert_reduce_fusion.3 = (f32[8,72]{1,0:T(8,128)}, bf16[2,8,368,72]{2,3,1,0:T(8,128)(2,1)S(1)}) fusion(bf16[2,8,368,736]{3,2,1,0:T(8,128)(2,1)} %copy-done.3, bf16[2,8,368,72]{2,3,0,1:T(8,128)(2,1)} %collective-permute-done.5, bf16[2,8,368,72]{2,3,0,1:T(8,128)(2,1)} %get-tuple-element.51), kind=kOutput, calls=%fused_computation.58 | convolution fusion | flops 629120448 | bytes 11213056 | tf_op jit(solution)/shard_map/bhqk,bhke->bhqe/dot_general | solution.py:219
  374.3 6.6 %bitcast_convert_fusion = bf16[1152,3,8,72]{0,3,2,1:T(8,128)(2,1)} fusion(bf16[1,368,1152]{2,1,0:T(8,128)(2,1)} %bitcast.18, bf16[1,368,1152]{2,1,0:T(8,128)(2,1)S(1)} %copy-done.32, bf16[1,2,8,368,72]{3,4,2,1,0:T(8,128)(2,1)S(1)} %get-tuple-element.48, bf16[1,2,8,368,72]{3,4,2,1,0:T(8,128)(2,1)S(1)} %fusion.70, bf16[1,2,8,368,72]{3,4,2,1,0:T(8,128)(2,1)S(1)} %bitcast.243), kind=kOutput, calls=%fused_computation.14 | convolution fusion | flops 2943258624 | bytes 8220672 | tf_op jit(solution)/shard_map/okz,toaks->ztas/dot_general | solution.py:230
  381.0 6.6 %copy.93 = bf16[1152,1728]{1,0:T(8,128)(2,1)} copy(bf16[1152,1728]{0,1:T(8,128)(2,1)} %bitcast.220) | data formatting | bytes 7962624 | tf_op jit(solution)/shard_map/convert_element_type | solution.py:235
  387.5 5.3 fusion.10
  394.4 6.3 %convolution_bitcast_fusion.1 = f32[2,368,1152]{2,1,0:T(8,128)S(1)} fusion(bf16[3,1152,8,72,1]{1,3,2,4,0:T(8,128)(2,1)} %bitcast.219, bf16[1,2,8,368,72]{3,4,2,1,0:T(8,128)(2,1)S(1)} %copy-done.28, bf16[1,2,8,368,72]{3,4,2,1,0:T(8,128)(2,1)S(1)} %copy-done.26, bf16[1,2,8,368,72]{3,4,2,1,0:T(8,128)(2,1)} %bitcast.244), kind=kOutput, calls=%fused_computation.32 | convolution fusion | flops 2932789248 | bytes 9916416 | tf_op jit(solution)/shard_map/toaks,tzas->okz/dot_general | solution.py:242
  406.1 18.2 %collective-permute-done.15 = bf16[368,1152]{1,0:T(8,128)(2,1)S(1)} collective-permute-done((bf16[368,1152]{1,0:T(8,128)(2,1)}, bf16[368,1152]{1,0:T(8,128)(2,1)S(1)}, u32[]{:S(2)}, u32[]{:S(2)}) %collective-permute-start.15) | collective-permute-done | bytes 847904 | tf_op jit(solution)/shard_map/ppermute | solution.py:46
  447.2 4.9 collective-permute-done.24
  457.9 17.1 %reduce-scatter.7.cloned.1.call-done = bf16[72,2368]{1,0:T(8,128)(2,1)} async-done(((bf16[1152,2368]{1,0:T(8,128)(2,1)}), bf16[72,2368]{1,0:T(8,128)(2,1)}) %reduce-scatter.7.cloned.1.call-update) | async-done | bytes 341008
  478.5 113.4 %reduce-scatter.5.cloned.1.call-done = bf16[72,4352]{1,0:T(8,128)(2,1)} async-done(((bf16[1152,4352]{1,0:T(8,128)(2,1)}), bf16[72,4352]{1,0:T(8,128)(2,1)}) %reduce-scatter.5.cloned.1.call-update) | async-done | bytes 626704 | tf_op jit(solution)/shard_map/reduce_scatter | solution.py:201
  (262 shorter events, 131.7 us)
Async XLA Ops:
  7.2 77.1 %all-gather.3.cloned.1.call-start = ((), (), s32[]{:S(2)}) async-start(), calls=%async_computation.2 | async-start | bytes 7833600 | tf_op jit(solution)/shard_map/all_gather | solution.py:132
  13.6 172.1 %all-gather.5.cloned.1.call-start = ((), (), s32[]{:S(2)}) async-start(), calls=%async_computation.3 | async-start | bytes 10653696 | tf_op jit(solution)/shard_map/all_gather | solution.py:134
  14.5 460.4 %reduce-scatter.7.cloned.1.call-start = ((), (), s32[]{:S(2)}) async-start(), calls=%async_computation.5 | async-start | bytes 5953536
  14.6 4.9 collective-permute-start
  20.0 3.7 collective-permute-start.1
  24.3 3.8 collective-permute-start.2
  28.7 5.0 collective-permute-start.3
  34.5 67.4 %copy-start.37 = (f32[368]{0:T(512)}, f32[368]{0:T(512)S(1)}, u32[]{:S(2)}) copy-start(f32[368]{0:T(512)S(1)} %broadcast_multiply_fusion.5) | copy-start | bytes 4420
  34.9 67.0 %copy-start.39 = (f32[368]{0:T(512)}, f32[368]{0:T(512)S(1)}, u32[]{:S(2)}) copy-start(f32[368]{0:T(512)S(1)} %add_rsqrt_fusion.1) | copy-start | bytes 4420
  88.6 21.2 %collective-permute-start.4 = (bf16[368,1152]{1,0:T(8,128)(2,1)S(1)}, bf16[368,1152]{1,0:T(8,128)(2,1)}, u32[]{:S(2)}, u32[]{:S(2)}) collective-permute-start(bf16[368,1152]{1,0:T(8,128)(2,1)S(1)} %fusion.27), channel_id=1, source_target_pairs={{0,1},{1,0},{2,3},{3,2},{4,5},{5,4},{6,7},{7,6},{8,9},{9,8},{10,11... | collective-permute-start | bytes 2543624 | tf_op jit(solution)/shard_map/ppermute | solution.py:46
  117.4 2.8 collective-permute-start.5
  119.2 11.3 %collective-permute-start.6 = (bf16[2,8,368,72]{2,3,0,1:T(8,128)(2,1)}, bf16[2,8,368,72]{2,3,0,1:T(8,128)(2,1)S(1)}, u32[]{:S(2)}, u32[]{:S(2)}) collective-permute-start(bf16[2,8,368,72]{2,3,0,1:T(8,128)(2,1)} %get-tuple-element.50), channel_id=1, source_target_pairs={{0,2},{2,0},{1,3},{3,1},{4,6},{6,4},{5,7},{7,5},{8,10},{10,8},{9,1... | collective-permute-start | bytes 2543624 | tf_op jit(solution)/shard_map/ppermute | solution.py:46
  142.0 21.0 %collective-permute-start.7 = (bf16[368,1152]{1,0:T(8,128)(2,1)S(1)}, bf16[368,1152]{1,0:T(8,128)(2,1)S(1)}, u32[]{:S(2)}, u32[]{:S(2)}) collective-permute-start(bf16[368,1152]{1,0:T(8,128)(2,1)S(1)} %fusion.71), channel_id=1, source_target_pairs={{0,1},{1,0},{2,3},{3,2},{4,5},{5,4},{6,7},{7,6},{8,9},{9,8},{10,11... | collective-permute-start | bytes 2543624 | tf_op jit(solution)/shard_map/ppermute | solution.py:46
  164.1 20.2 %collective-permute-start.8 = (bf16[368,1152]{1,0:T(8,128)(2,1)S(1)}, bf16[368,1152]{1,0:T(8,128)(2,1)S(1)}, u32[]{:S(2)}, u32[]{:S(2)}) collective-permute-start(bf16[368,1152]{1,0:T(8,128)(2,1)S(1)} %add_convert_fusion.1), channel_id=1, source_target_pairs={{0,1},{1,0},{2,3},{3,2},{4,5},{5,4},{6,7},{7,6},{8,9},{9,8},{10,11... | collective-permute-start | bytes 2543624 | tf_op jit(solution)/shard_map/ppermute | solution.py:46
  201.9 19.6 %collective-permute-start.9 = (bf16[368,1152]{1,0:T(8,128)(2,1)}, bf16[368,1152]{1,0:T(8,128)(2,1)}, u32[]{:S(2)}, u32[]{:S(2)}) collective-permute-start(bf16[368,1152]{1,0:T(8,128)(2,1)} %slice.279), channel_id=1, source_target_pairs={{0,1},{1,0},{2,3},{3,2},{4,5},{5,4},{6,7},{7,6},{8,9},{9,8},{10,11... | collective-permute-start | bytes 2543624 | tf_op jit(solution)/shard_map/ppermute | solution.py:46
  225.1 18.5 %collective-permute-start.10 = (bf16[368,1152]{1,0:T(8,128)(2,1)S(1)}, bf16[368,1152]{1,0:T(8,128)(2,1)S(1)}, u32[]{:S(2)}, u32[]{:S(2)}) collective-permute-start(bf16[368,1152]{1,0:T(8,128)(2,1)S(1)} %multiply_convert_fusion.3), channel_id=1, source_target_pairs={{0,1},{1,0},{2,3},{3,2},{4,5},{5,4},{6,7},{7,6},{8,9},{9,8},{10,11... | collective-permute-start | bytes 2543624 | tf_op jit(solution)/shard_map/ppermute | solution.py:46
  271.1 17.9 %collective-permute-start.11 = (bf16[368,1152]{1,0:T(8,128)(2,1)}, bf16[368,1152]{1,0:T(8,128)(2,1)}, u32[]{:S(2)}, u32[]{:S(2)}) collective-permute-start(bf16[368,1152]{1,0:T(8,128)(2,1)} %slice.278), channel_id=1, source_target_pairs={{0,1},{1,0},{2,3},{3,2},{4,5},{5,4},{6,7},{7,6},{8,9},{9,8},{10,11... | collective-permute-start | bytes 2543624 | tf_op jit(solution)/shard_map/ppermute | solution.py:46
  295.7 16.8 %collective-permute-start.12 = (bf16[368,1152]{1,0:T(8,128)(2,1)S(1)}, bf16[368,1152]{1,0:T(8,128)(2,1)S(1)}, u32[]{:S(2)}, u32[]{:S(2)}) collective-permute-start(bf16[368,1152]{1,0:T(8,128)(2,1)S(1)} %convert_element_type.165), channel_id=1, source_target_pairs={{0,1},{1,0},{2,3},{3,2},{4,5},{5,4},{6,7},{7,6},{8,9},{9,8},{10,11... | collective-permute-start | bytes 2543624 | tf_op jit(solution)/shard_map/ppermute | solution.py:46
  325.4 46.2 %collective-permute-start.14 = (bf16[2,8,368,72]{2,3,1,0:T(8,128)(2,1)}, bf16[2,8,368,72]{2,3,1,0:T(8,128)(2,1)}, u32[]{:S(2)}, u32[]{:S(2)}) collective-permute-start(bf16[2,8,368,72]{2,3,1,0:T(8,128)(2,1)} %slice.276), channel_id=1, source_target_pairs={{0,2},{2,0},{1,3},{3,1},{4,6},{6,4},{5,7},{7,5},{8,10},{10,8},{9,1... | collective-permute-start | bytes 2543624 | tf_op jit(solution)/shard_map/ppermute | solution.py:46
  363.5 10.6 %collective-permute-start.13 = (bf16[2,8,368,72]{2,3,1,0:T(8,128)(2,1)S(1)}, bf16[2,8,368,72]{2,3,1,0:T(8,128)(2,1)S(1)}, u32[]{:S(2)}, u32[]{:S(2)}) collective-permute-start(bf16[2,8,368,72]{2,3,1,0:T(8,128)(2,1)S(1)} %slice.277), channel_id=1, source_target_pairs={{0,2},{2,0},{1,3},{3,1},{4,6},{6,4},{5,7},{7,5},{8,10},{10,8},{9,1... | collective-permute-start | bytes 2543624 | tf_op jit(solution)/shard_map/ppermute | solution.py:46
  392.9 199.0 %reduce-scatter.5.cloned.1.call-start = ((), (), s32[]{:S(2)}) async-start(), calls=%async_computation.4 | async-start | bytes 10653696 | tf_op jit(solution)/shard_map/reduce_scatter | solution.py:201
  394.3 29.9 %copy-start.40 = (f32[368]{0:T(512)S(1)}, f32[368]{0:T(512)}, u32[]{:S(2)}) copy-start(f32[368]{0:T(512)} %copy-done.39) | copy-start | bytes 4420
  403.4 20.9 %collective-permute-start.15 = (bf16[368,1152]{1,0:T(8,128)(2,1)}, bf16[368,1152]{1,0:T(8,128)(2,1)S(1)}, u32[]{:S(2)}, u32[]{:S(2)}) collective-permute-start(bf16[368,1152]{1,0:T(8,128)(2,1)} %fusion.72), channel_id=1, source_target_pairs={{0,1},{1,0},{2,3},{3,2},{4,5},{5,4},{6,7},{7,6},{8,9},{9,8},{10,11... | collective-permute-start | bytes 2543624 | tf_op jit(solution)/shard_map/ppermute | solution.py:46
  428.8 1.3 collective-permute-start.16
  430.1 4.6 collective-permute-start.17
  434.7 3.9 collective-permute-start.18
  436.5 1.2 collective-permute-start.21
  437.7 3.7 collective-permute-start.22
  438.5 13.6 %collective-permute-start.19 = (f32[6913]{0:T(1024)S(1)}, f32[6913]{0:T(1024)S(1)}, u32[]{:S(2)}, u32[]{:S(2)}) collective-permute-start(f32[6913]{0:T(1024)S(1)} %add.281), channel_id=1, source_target_pairs={{0,16},{4,20},{8,24},{12,28},{16,0},{20,4},{24,8},{28,12},{1,17},{... | collective-permute-start | bytes 82964 | tf_op jit(solution)/shard_map/ppermute | solution.py:93
  441.4 5.2 collective-permute-start.23
  446.7 5.4 collective-permute-start.24
  452.1 3.9 collective-permute-start.20
  (54 other events, 529.6 us)
Sparse Core Ops, SparseCore 0:
  13.7 70.5 all-gather.2
  87.1 83.4 all-gather.4
  393.0 81.8 reduce-scatter.6
  478.9 112.8 reduce-scatter.4
where the time goes:
time: 608 us; the launch traced here: 603 us
  waiting for transfers between devices  326 us (54%)
  matrix products  109 us (18%)
  local copies, waits for them, and re-layouts  58.2 us (10%)
  other arithmetic  54 us (9%)
  starting transfers between devices  35.7 us (6%)
  between operations  20.7 us (3%)
    ppermute x12, waiting for transfers between devices, swap(): return lax.ppermute(values, axis, [(0, 1), (1, 0)])  126 us
    reduce_scatter x1, waiting for transfers between devices, on_device(): lax.psum_scatter(mlp_grad_pack, ('dp', 'ctx'), scatter_dimension=0, tiled...  113 us
    all_gather x1, waiting for transfers between devices, on_device(): attn_full = lax.all_gather(attn_pack, ('dp', 'ctx'), axis=1, tiled=True)  49.4 us
    ppermute x13, starting transfers between devices, tree_sum(): values = jax.tree.map(lambda v: v + lax.ppermute(v, axis, perm), values)  22.5 us
    ppermute x13, waiting for transfers between devices, tree_sum(): values = jax.tree.map(lambda v: v + lax.ppermute(v, axis, perm), values)  19.3 us
    unnamed x5, waiting for transfers between devices  17.6 us
    unnamed x128, local copies, waits for them, and re-layouts  16.5 us
    dot_general x1, matrix products, on_device(): jnp.einsum('bhqe,bhke->bhqk', mixed_grad, value_all, preferred_element_ty...  14.7 us
  transfers between devices with their start and end apart: 29, of which 23 were waited for; matrix products, arithmetic and copies ran while one was open for 20% of the time, Pallas kernels for 0%

commit v1 on v0

--- a/solution.py
+++ b/solution.py
@@ -129,7 +129,29 @@
     vector_rows = jnp.stack([ln1_gain, ln1_bias, b_o, ln2_gain, ln2_bias, b_down], axis=1)
     vector_slot = jnp.pad(vector_rows, ((0, 0), (0, head_width - vector_rows.shape[1])))
     attn_pack = jnp.stack([w_q, w_k, w_v, w_o.T, vector_slot])
-    attn_full = lax.all_gather(attn_pack, ("dp", "ctx"), axis=1, tiled=True)
+    count, index, span = (
+        lax.axis_size(("dp", "ctx")),
+        lax.axis_index(("dp", "ctx")),
+        attn_pack.shape[1],
+    )
+    right = [(i_2, (i_2 + 1) % count) for i_2 in range(count)]
+    left = [(i_2, (i_2 - 1) % count) for i_2 in range(count)]
+    attn_full = jnp.zeros(
+        (*attn_pack.shape[:1], count * span, *attn_pack.shape[1 + 1 :]), attn_pack.dtype
+    )
+    attn_full = lax.dynamic_update_slice_in_dim(attn_full, attn_pack, index * span, axis=1)
+    from_left = from_right = attn_pack
+    half = count // 2
+    for k in range(1, half + 1):
+        from_left = lax.ppermute(from_left, ("dp", "ctx"), right)
+        attn_full = lax.dynamic_update_slice_in_dim(
+            attn_full, from_left, (index - k) % count * span, axis=1
+        )
+        if k < count - half:
+            from_right = lax.ppermute(from_right, ("dp", "ctx"), left)
+            attn_full = lax.dynamic_update_slice_in_dim(
+                attn_full, from_right, (index + k) % count * span, axis=1
+            )
     mlp_pack = jnp.pad(jnp.stack([w_up, w_down.T]), ((0, 0), (0, 0), (0, pad_hidden)))
     mlp_full = lax.all_gather(mlp_pack, ("dp", "ctx"), axis=1, tiled=True)
     qkv_w = attn_full[:3].reshape(3, width, local_heads, HD)

time: 608 us -> 896 us (1.47); the launches traced: 603 us -> 880 us
  local copies, waits for them, and re-layouts: 58.2 us -> 274 us
  starting transfers between devices: 35.7 us -> 77.6 us
  waiting for transfers between devices: 326 us -> 347 us
    dynamic_update_slice x0 -> x16, local copies, waits for them, and re-layouts: none -> 214 us  [the longest x8 108 us: on_device(): lax.dynamic_update_slice_in_dim(attn_full, from_left, (index - k) % count...]
    ppermute x0 -> x15, waiting for transfers between devices: none -> 57 us  [the longest x7 41 us: on_device(): from_right = lax.ppermute(from_right, ('dp', 'ctx'), left)]
    all_gather x1 -> x0, waiting for transfers between devices: 49.4 us -> none  [on_device(): attn_full = lax.all_gather(attn_pack, ('dp', 'ctx'), axis=1, tiled=True)]
    ppermute x0 -> x15, starting transfers between devices: none -> 45.4 us  [the longest x7 28.3 us: on_device(): from_right = lax.ppermute(from_right, ('dp', 'ctx'), left)]
    ppermute x12, waiting for transfers between devices: 126 us -> 138 us  [swap(): return lax.ppermute(values, axis, [(0, 1), (1, 0)])]
    ppermute x0 -> x15, local copies, waits for them, and re-layouts: none -> 10.5 us  [the longest x7 5.59 us: on_device(): from_right = lax.ppermute(from_right, ('dp', 'ctx'), left)]
    slice x2 -> x1, local copies, waits for them, and re-layouts: 11.4 us -> 2.43 us  [on_device(): qkv_w = attn_full[:3].reshape(3, width, local_heads, HD)]
  transfers between devices with their start and end apart: 29 -> 43, of which waited for: 23 -> 32; matrix products, arithmetic and copies ran while one was open for 20% -> 38% of each run, Pallas kernels for 0% -> 0%
where the time goes in v1:
time: 896 us; the launch traced here: 880 us
  waiting for transfers between devices  347 us (39%)
  local copies, waits for them, and re-layouts  274 us (31%)
  matrix products  106 us (12%)
  starting transfers between devices  77.6 us (9%)
  other arithmetic  54.9 us (6%)
  between operations  20.5 us (2%)
    ppermute x12, waiting for transfers between devices, swap(): return lax.ppermute(values, axis, [(0, 1), (1, 0)])  138 us
    reduce_scatter x1, waiting for transfers between devices, on_device(): lax.psum_scatter(mlp_grad_pack, ('dp', 'ctx'), scatter_dimension=0, tiled...  114 us
    dynamic_update_slice x8, local copies, waits for them, and re-layouts, on_device(): lax.dynamic_update_slice_in_dim(attn_full, from_left, (index - k) % count...  108 us
    dynamic_update_slice x7, local copies, waits for them, and re-layouts, on_device(): lax.dynamic_update_slice_in_dim(attn_full, from_right, (index + k) % coun...  94.7 us
    ppermute x7, waiting for transfers between devices, on_device(): from_right = lax.ppermute(from_right, ('dp', 'ctx'), left)  41 us
    ppermute x7, starting transfers between devices, on_device(): from_right = lax.ppermute(from_right, ('dp', 'ctx'), left)  28.3 us
    ppermute x13, starting transfers between devices, tree_sum(): values = jax.tree.map(lambda v: v + lax.ppermute(v, axis, perm), values)  21.3 us
    ppermute x13, waiting for transfers between devices, tree_sum(): values = jax.tree.map(lambda v: v + lax.ppermute(v, axis, perm), values)  21.2 us
  transfers between devices with their start and end apart: 43, of which 32 were waited for; matrix products, arithmetic and copies ran while one was open for 38% of the time, Pallas kernels for 0%

profile of v1, /device:TPU:0, one launch (start us, length us, event | category | flops | bytes accessed | tf_op | source)
XLA Modules:
  0.0 880.1 jit_solution(6072038745289855896)
XLA Ops:
  38.4 8.7 collective-permute-done.6
  57.8 15.5 %collective-permute-done.9 = bf16[5,72,576]{2,1,0:T(8,128)(2,1)S(1)} collective-permute-done((bf16[5,72,576]{2,1,0:T(8,128)(2,1)S(1)}, bf16[5,72,576]{2,1,0:T(8,128)(2,1)S(1)}, u32[]{:S(2)}, u32[]{:S(2)}) %collective-permute-start.9) | collective-permute-done | bytes 414752 | tf_op jit(solution)/shard_map/ppermute | solution.py:151
  78.2 12.7 %collective-permute-done.11 = bf16[5,72,576]{2,1,0:T(8,128)(2,1)S(1)} collective-permute-done((bf16[5,72,576]{2,1,0:T(8,128)(2,1)S(1)}, bf16[5,72,576]{2,1,0:T(8,128)(2,1)S(1)}, u32[]{:S(2)}, u32[]{:S(2)}) %collective-permute-start.11) | collective-permute-done | bytes 414752 | tf_op jit(solution)/shard_map/ppermute | solution.py:151
  121.4 11.8 %dynamic_update_slice.48 = bf16[5,1152,576]{1,2,0:T(8,128)(2,1)} dynamic-update-slice(bf16[5,1152,576]{1,2,0:T(8,128)(2,1)} %broadcast_in_dim.21, bf16[5,72,576]{1,2,0:T(8,128)(2,1)S(1)} %bitcast_dynamic-update-slice_fusion.1, s32[]{:T(128)} %constant.149.clone.1, s32[]{:T(128)S(6)} %select_n.145, s32[]{:T(128)} %constant.149.clone.1) | dynamic-update-slice | bytes 829444 | tf_op jit(solution)/shard_map/dynamic_update_slice | solution.py:142
  152.2 13.1 %dynamic_update_slice.49 = bf16[5,1152,576]{1,2,0:T(8,128)(2,1)} dynamic-update-slice(bf16[5,1152,576]{1,2,0:T(8,128)(2,1)} %dynamic_update_slice.48, bf16[5,72,576]{1,2,0:T(8,128)(2,1)S(1)} %copy.59, s32[]{:T(128)} %constant.149.clone.1, s32[]{:T(128)S(6)} %select_n.147, s32[]{:T(128)} %constant.149.clone.1) | dynamic-update-slice | bytes 829444 | tf_op jit(solution)/shard_map/dynamic_update_slice | solution.py:147
  165.6 13.5 %dynamic_update_slice.50 = bf16[5,1152,576]{1,2,0:T(8,128)(2,1)} dynamic-update-slice(bf16[5,1152,576]{1,2,0:T(8,128)(2,1)} %dynamic_update_slice.49, bf16[5,72,576]{1,2,0:T(8,128)(2,1)S(1)} %copy.61, s32[]{:T(128)} %constant.149.clone.1, s32[]{:T(128)S(6)} %select_n.149, s32[]{:T(128)} %constant.149.clone.1) | dynamic-update-slice | bytes 829444 | tf_op jit(solution)/shard_map/dynamic_update_slice | solution.py:152
  179.5 13.6 %dynamic_update_slice.51 = bf16[5,1152,576]{1,2,0:T(8,128)(2,1)} dynamic-update-slice(bf16[5,1152,576]{1,2,0:T(8,128)(2,1)} %dynamic_update_slice.50, bf16[5,72,576]{1,2,0:T(8,128)(2,1)S(1)} %copy.62, s32[]{:T(128)} %constant.149.clone.1, s32[]{:T(128)S(6)} %select_n.151, s32[]{:T(128)} %constant.149.clone.1) | dynamic-update-slice | bytes 829444 | tf_op jit(solution)/shard_map/dynamic_update_slice | solution.py:147
  193.4 13.6 %dynamic_update_slice.52 = bf16[5,1152,576]{1,2,0:T(8,128)(2,1)} dynamic-update-slice(bf16[5,1152,576]{1,2,0:T(8,128)(2,1)} %dynamic_update_slice.51, bf16[5,72,576]{1,2,0:T(8,128)(2,1)S(1)} %copy.63, s32[]{:T(128)} %constant.149.clone.1, s32[]{:T(128)S(6)} %select_n.153, s32[]{:T(128)} %constant.149.clone.1) | dynamic-update-slice | bytes 829444 | tf_op jit(solution)/shard_map/dynamic_update_slice | solution.py:152
  207.4 13.6 %dynamic_update_slice.53 = bf16[5,1152,576]{1,2,0:T(8,128)(2,1)} dynamic-update-slice(bf16[5,1152,576]{1,2,0:T(8,128)(2,1)} %dynamic_update_slice.52, bf16[5,72,576]{1,2,0:T(8,128)(2,1)S(1)} %copy.64, s32[]{:T(128)} %constant.149.clone.1, s32[]{:T(128)S(6)} %select_n.155, s32[]{:T(128)} %constant.149.clone.1) | dynamic-update-slice | bytes 829444 | tf_op jit(solution)/shard_map/dynamic_update_slice | solution.py:147
  221.3 13.6 %dynamic_update_slice.54 = bf16[5,1152,576]{1,2,0:T(8,128)(2,1)} dynamic-update-slice(bf16[5,1152,576]{1,2,0:T(8,128)(2,1)} %dynamic_update_slice.53, bf16[5,72,576]{1,2,0:T(8,128)(2,1)S(1)} %copy.65, s32[]{:T(128)} %constant.149.clone.1, s32[]{:T(128)S(6)} %select_n.157, s32[]{:T(128)} %constant.149.clone.1) | dynamic-update-slice | bytes 829444 | tf_op jit(solution)/shard_map/dynamic_update_slice | solution.py:152
  235.2 13.5 %dynamic_update_slice.55 = bf16[5,1152,576]{1,2,0:T(8,128)(2,1)} dynamic-update-slice(bf16[5,1152,576]{1,2,0:T(8,128)(2,1)} %dynamic_update_slice.54, bf16[5,72,576]{1,2,0:T(8,128)(2,1)S(1)} %copy.66, s32[]{:T(128)} %constant.149.clone.1, s32[]{:T(128)S(6)} %select_n.159, s32[]{:T(128)} %constant.149.clone.1) | dynamic-update-slice | bytes 829444 | tf_op jit(solution)/shard_map/dynamic_update_slice | solution.py:147
  249.1 13.5 %dynamic_update_slice.56 = bf16[5,1152,576]{1,2,0:T(8,128)(2,1)} dynamic-update-slice(bf16[5,1152,576]{1,2,0:T(8,128)(2,1)} %dynamic_update_slice.55, bf16[5,72,576]{1,2,0:T(8,128)(2,1)S(1)} %copy.67, s32[]{:T(128)} %constant.149.clone.1, s32[]{:T(128)S(6)} %select_n.161, s32[]{:T(128)} %constant.149.clone.1) | dynamic-update-slice | bytes 829444 | tf_op jit(solution)/shard_map/dynamic_update_slice | solution.py:152
  263.0 13.5 %dynamic_update_slice.57 = bf16[5,1152,576]{1,2,0:T(8,128)(2,1)} dynamic-update-slice(bf16[5,1152,576]{1,2,0:T(8,128)(2,1)} %dynamic_update_slice.56, bf16[5,72,576]{1,2,0:T(8,128)(2,1)S(1)} %copy.68, s32[]{:T(128)} %constant.149.clone.1, s32[]{:T(128)S(6)} %select_n.163, s32[]{:T(128)} %constant.149.clone.1) | dynamic-update-slice | bytes 829444 | tf_op jit(solution)/shard_map/dynamic_update_slice | solution.py:147
  277.9 13.5 %dynamic_update_slice.58 = bf16[5,1152,576]{1,2,0:T(8,128)(2,1)} dynamic-update-slice(bf16[5,1152,576]{1,2,0:T(8,128)(2,1)} %dynamic_update_slice.57, bf16[5,72,576]{1,2,0:T(8,128)(2,1)S(1)} %copy.69, s32[]{:T(128)} %constant.149.clone.1, s32[]{:T(128)S(6)} %select_n.165, s32[]{:T(128)} %constant.149.clone.1) | dynamic-update-slice | bytes 829444 | tf_op jit(solution)/shard_map/dynamic_update_slice | solution.py:152
  292.9 13.5 %dynamic_update_slice.59 = bf16[5,1152,576]{1,2,0:T(8,128)(2,1)} dynamic-update-slice(bf16[5,1152,576]{1,2,0:T(8,128)(2,1)} %dynamic_update_slice.58, bf16[5,72,576]{1,2,0:T(8,128)(2,1)S(1)} %copy.70, s32[]{:T(128)} %constant.149.clone.1, s32[]{:T(128)S(6)} %select_n.167, s32[]{:T(128)} %constant.149.clone.1) | dynamic-update-slice | bytes 829444 | tf_op jit(solution)/shard_map/dynamic_update_slice | solution.py:147
  307.7 13.5 %dynamic_update_slice.60 = bf16[5,1152,576]{1,2,0:T(8,128)(2,1)} dynamic-update-slice(bf16[5,1152,576]{1,2,0:T(8,128)(2,1)} %dynamic_update_slice.59, bf16[5,72,576]{1,2,0:T(8,128)(2,1)S(1)} %copy.71, s32[]{:T(128)} %constant.149.clone.1, s32[]{:T(128)S(6)} %select_n.169, s32[]{:T(128)} %constant.149.clone.1) | dynamic-update-slice | bytes 829444 | tf_op jit(solution)/shard_map/dynamic_update_slice | solution.py:152
  321.6 13.5 %dynamic_update_slice.61 = bf16[5,1152,576]{1,2,0:T(8,128)(2,1)} dynamic-update-slice(bf16[5,1152,576]{1,2,0:T(8,128)(2,1)} %dynamic_update_slice.60, bf16[5,72,576]{1,2,0:T(8,128)(2,1)S(1)} %copy.72, s32[]{:T(128)} %constant.149.clone.1, s32[]{:T(128)S(6)} %select_n.171, s32[]{:T(128)} %constant.149.clone.1) | dynamic-update-slice | bytes 829444 | tf_op jit(solution)/shard_map/dynamic_update_slice | solution.py:147
  336.5 13.5 %dynamic_update_slice.62 = bf16[5,1152,576]{1,2,0:T(8,128)(2,1)} dynamic-update-slice(bf16[5,1152,576]{1,2,0:T(8,128)(2,1)} %dynamic_update_slice.61, bf16[5,72,576]{1,2,0:T(8,128)(2,1)S(1)} %copy.73, s32[]{:T(128)} %constant.149.clone.1, s32[]{:T(128)S(6)} %select_n.173, s32[]{:T(128)} %constant.149.clone.1) | dynamic-update-slice | bytes 829444 | tf_op jit(solution)/shard_map/dynamic_update_slice | solution.py:152
  351.4 13.6 %dynamic_update_slice.63 = bf16[5,1152,576]{1,2,0:T(8,128)(2,1)} dynamic-update-slice(bf16[5,1152,576]{1,2,0:T(8,128)(2,1)} %dynamic_update_slice.62, bf16[5,72,576]{1,2,0:T(8,128)(2,1)S(1)} %copy.74, s32[]{:T(128)} %constant.149.clone.1, s32[]{:T(128)S(6)} %select_n.175, s32[]{:T(128)} %constant.149.clone.1) | dynamic-update-slice | bytes 829444 | tf_op jit(solution)/shard_map/dynamic_update_slice | solution.py:147
  372.9 16.1 %collective-permute-done.19 = bf16[368,1152]{1,0:T(8,128)(2,1)S(1)} collective-permute-done((bf16[368,1152]{1,0:T(8,128)(2,1)S(1)}, bf16[368,1152]{1,0:T(8,128)(2,1)S(1)}, u32[]{:S(2)}, u32[]{:S(2)}) %collective-permute-start.19) | collective-permute-done | bytes 847904 | tf_op jit(solution)/shard_map/ppermute | solution.py:46
  420.4 19.7 %collective-permute-done.22 = bf16[368,1152]{1,0:T(8,128)(2,1)S(1)} collective-permute-done((bf16[368,1152]{1,0:T(8,128)(2,1)S(1)}, bf16[368,1152]{1,0:T(8,128)(2,1)S(1)}, u32[]{:S(2)}, u32[]{:S(2)}) %collective-permute-start.22) | collective-permute-done | bytes 847904 | tf_op jit(solution)/shard_map/ppermute | solution.py:46
  442.8 18.5 %collective-permute-done.23 = bf16[368,1152]{1,0:T(8,128)(2,1)S(1)} collective-permute-done((bf16[368,1152]{1,0:T(8,128)(2,1)S(1)}, bf16[368,1152]{1,0:T(8,128)(2,1)S(1)}, u32[]{:S(2)}, u32[]{:S(2)}) %collective-permute-start.23) | collective-permute-done | bytes 847904 | tf_op jit(solution)/shard_map/ppermute | solution.py:46
  480.1 18.3 %collective-permute-done.24 = bf16[368,1152]{1,0:T(8,128)(2,1)} collective-permute-done((bf16[368,1152]{1,0:T(8,128)(2,1)}, bf16[368,1152]{1,0:T(8,128)(2,1)}, u32[]{:S(2)}, u32[]{:S(2)}) %collective-permute-start.24) | collective-permute-done | bytes 847904 | tf_op jit(solution)/shard_map/ppermute | solution.py:46
  503.5 17.2 %collective-permute-done.25 = bf16[368,1152]{1,0:T(8,128)(2,1)S(1)} collective-permute-done((bf16[368,1152]{1,0:T(8,128)(2,1)S(1)}, bf16[368,1152]{1,0:T(8,128)(2,1)S(1)}, u32[]{:S(2)}, u32[]{:S(2)}) %collective-permute-start.25) | collective-permute-done | bytes 847904 | tf_op jit(solution)/shard_map/ppermute | solution.py:46
  526.5 9.5 %fusion.9 = bf16[736,2176]{1,0:T(8,128)(2,1)S(1)} fusion(bf16[736,1152]{1,0:T(8,128)(2,1)S(1)} %bitcast.226, f32[736,2176]{1,0:T(8,128)} %copy-done.63, bf16[2,1152,2176]{2,1,0:T(8,128)(2,1)S(1)} %bitcast.241, f32[2176]{0:T(1024)S(1)} %pad_convert_fusion), kind=kOutput, calls=%fused_computation.21 | convolution fusion | flops 3721969664 | bytes 16330752 | tf_op jit(solution)/shard_map/rd,df->rf/dot_general | solution.py:211
  553.9 12.0 %collective-permute-done.26 = bf16[368,1152]{1,0:T(8,128)(2,1)} collective-permute-done((bf16[368,1152]{1,0:T(8,128)(2,1)}, bf16[368,1152]{1,0:T(8,128)(2,1)}, u32[]{:S(2)}, u32[]{:S(2)}) %collective-permute-start.26) | collective-permute-done | bytes 847904 | tf_op jit(solution)/shard_map/ppermute | solution.py:46
  574.0 15.3 %collective-permute-done.27 = bf16[368,1152]{1,0:T(8,128)(2,1)S(1)} collective-permute-done((bf16[368,1152]{1,0:T(8,128)(2,1)S(1)}, bf16[368,1152]{1,0:T(8,128)(2,1)S(1)}, u32[]{:S(2)}, u32[]{:S(2)}) %collective-permute-start.27) | collective-permute-done | bytes 847904 | tf_op jit(solution)/shard_map/ppermute | solution.py:46
  602.2 14.6 %multiply_reduce_fusion = (f32[2,8,368]{2,1,0:T(8,128)S(1)}, f32[2,8,368,736]{3,2,1,0:T(8,128)}) fusion(f32[2,8,368,736]{3,2,1,0:T(8,128)} %copy-done, f32[2,8,368]{2,1,0:T(8,128)S(1)} %log_add_fusion, pred[736]{0:T(1024)(128)(4,1)S(1)} %fusion.82, bf16[2,8,368,72]{2,3,0,1:T(8,128)(2,1)S(1)} %fusion.65, bf16[2,8,368,72]{2,3,0,1:T(8,128)(2,1)S(1)} %copy-done.30, ...), kind=kOutput, calls=%fused_computation.1 | convolution fusion | flops 649087232 | bytes 37260000 | tf_op jit(solution)/shard_map/bhqe,bhke->bhqk/dot_general | solution.py:234
  616.8 12.9 %multiply_convert_fusion = bf16[2,8,368,736]{3,2,1,0:T(8,128)(2,1)S(1)} fusion(f32[2,8,368,736]{3,2,1,0:T(8,128)} %get-tuple-element.70, f32[2,8,368,736]{3,2,1,0:T(8,128)} %copy-done, f32[2,8,368]{2,1,0:T(8,128)S(1)} %get-tuple-element.69, f32[2,8,368]{2,1,0:T(8,128)S(1)} %log_add_fusion, pred[736]{0:T(1024)(128)(4,1)S(1)} %fusion.82), kind=kLoop, calls=%fused_computation | loop fusion | flops 26001408 | bytes 43383520 | tf_op jit(solution)/shard_map/convert_element_type | solution.py:239
  682.0 18.4 %collective-permute-done.30 = bf16[368,1152]{1,0:T(8,128)(2,1)S(1)} collective-permute-done((bf16[368,1152]{1,0:T(8,128)(2,1)}, bf16[368,1152]{1,0:T(8,128)(2,1)S(1)}, u32[]{:S(2)}, u32[]{:S(2)}) %collective-permute-start.30) | collective-permute-done | bytes 847904 | tf_op jit(solution)/shard_map/ppermute | solution.py:46
  735.5 16.5 %reduce-scatter.7.cloned.1.call-done = bf16[72,2368]{1,0:T(8,128)(2,1)} async-done(((bf16[1152,2368]{1,0:T(8,128)(2,1)}), bf16[72,2368]{1,0:T(8,128)(2,1)}) %reduce-scatter.7.cloned.1.call-update) | async-done | bytes 341008
  755.6 113.6 %reduce-scatter.5.cloned.1.call-done = bf16[72,4352]{1,0:T(8,128)(2,1)} async-done(((bf16[1152,4352]{1,0:T(8,128)(2,1)}), bf16[72,4352]{1,0:T(8,128)(2,1)}) %reduce-scatter.5.cloned.1.call-update) | async-done | bytes 626704 | tf_op jit(solution)/shard_map/reduce_scatter | solution.py:223
  (343 shorter events, 305.7 us)
Async XLA Ops:
  7.2 455.5 %all-gather.2.cloned.1.call-start = ((), (), s32[]{:S(2)}) async-start(), calls=%async_computation.2 | async-start | bytes 10653696 | tf_op jit(solution)/shard_map/all_gather | solution.py:156
  9.2 742.9 %reduce-scatter.7.cloned.1.call-start = ((), (), s32[]{:S(2)}) async-start(), calls=%async_computation.4 | async-start | bytes 5953536
  14.7 11.8 %collective-permute-start.4 = (bf16[5,72,576]{2,1,0:T(8,128)(2,1)S(1)}, bf16[5,72,576]{2,1,0:T(8,128)(2,1)S(1)}, u32[]{:S(2)}, u32[]{:S(2)}) collective-permute-start(bf16[5,72,576]{2,1,0:T(8,128)(2,1)S(1)} %copy.58), channel_id=1, source_target_pairs={{0,2},{2,4},{4,6},{6,8},{8,10},{10,12},{12,14},{14,16},{16,18},{18... | collective-permute-start | bytes 1244168 | tf_op jit(solution)/shard_map/ppermute | solution.py:146
  15.2 18.5 %collective-permute-start.5 = (bf16[5,72,576]{2,1,0:T(8,128)(2,1)S(1)}, bf16[5,72,576]{2,1,0:T(8,128)(2,1)S(1)}, u32[]{:S(2)}, u32[]{:S(2)}) collective-permute-start(bf16[5,72,576]{2,1,0:T(8,128)(2,1)S(1)} %copy.58), channel_id=1, source_target_pairs={{0,30},{2,0},{4,2},{6,4},{8,6},{10,8},{12,10},{14,12},{16,14},{18,... | collective-permute-start | bytes 1244168 | tf_op jit(solution)/shard_map/ppermute | solution.py:151
  26.5 20.5 %collective-permute-start.6 = (bf16[5,72,576]{2,1,0:T(8,128)(2,1)S(1)}, bf16[5,72,576]{2,1,0:T(8,128)(2,1)S(1)}, u32[]{:S(2)}, u32[]{:S(2)}) collective-permute-start(bf16[5,72,576]{2,1,0:T(8,128)(2,1)S(1)} %collective-permute-done.4), channel_id=1, source_target_pairs={{0,2},{2,4},{4,6},{6,8},{8,10},{10,12},{12,14},{14,16},{16,18},{18... | collective-permute-start | bytes 1244168 | tf_op jit(solution)/shard_map/ppermute | solution.py:146
  33.8 19.1 %collective-permute-start.7 = (bf16[5,72,576]{2,1,0:T(8,128)(2,1)S(1)}, bf16[5,72,576]{2,1,0:T(8,128)(2,1)S(1)}, u32[]{:S(2)}, u32[]{:S(2)}) collective-permute-start(bf16[5,72,576]{2,1,0:T(8,128)(2,1)S(1)} %collective-permute-done.5), channel_id=1, source_target_pairs={{0,30},{2,0},{4,2},{6,4},{8,6},{10,8},{12,10},{14,12},{16,14},{18,... | collective-permute-start | bytes 1244168 | tf_op jit(solution)/shard_map/ppermute | solution.py:151
  47.0 10.7 %collective-permute-start.8 = (bf16[5,72,576]{2,1,0:T(8,128)(2,1)S(1)}, bf16[5,72,576]{2,1,0:T(8,128)(2,1)S(1)}, u32[]{:S(2)}, u32[]{:S(2)}) collective-permute-start(bf16[5,72,576]{2,1,0:T(8,128)(2,1)S(1)} %collective-permute-done.6), channel_id=1, source_target_pairs={{0,2},{2,4},{4,6},{6,8},{8,10},{10,12},{12,14},{14,16},{16,18},{18... | collective-permute-start | bytes 1244168 | tf_op jit(solution)/shard_map/ppermute | solution.py:146
  52.8 20.4 %collective-permute-start.9 = (bf16[5,72,576]{2,1,0:T(8,128)(2,1)S(1)}, bf16[5,72,576]{2,1,0:T(8,128)(2,1)S(1)}, u32[]{:S(2)}, u32[]{:S(2)}) collective-permute-start(bf16[5,72,576]{2,1,0:T(8,128)(2,1)S(1)} %collective-permute-done.7), channel_id=1, source_target_pairs={{0,30},{2,0},{4,2},{6,4},{8,6},{10,8},{12,10},{14,12},{16,14},{18,... | collective-permute-start | bytes 1244168 | tf_op jit(solution)/shard_map/ppermute | solution.py:151
  57.8 20.4 %collective-permute-start.10 = (bf16[5,72,576]{2,1,0:T(8,128)(2,1)S(1)}, bf16[5,72,576]{2,1,0:T(8,128)(2,1)S(1)}, u32[]{:S(2)}, u32[]{:S(2)}) collective-permute-start(bf16[5,72,576]{2,1,0:T(8,128)(2,1)S(1)} %collective-permute-done.8), channel_id=1, source_target_pairs={{0,2},{2,4},{4,6},{6,8},{8,10},{10,12},{12,14},{14,16},{16,18},{18... | collective-permute-start | bytes 1244168 | tf_op jit(solution)/shard_map/ppermute | solution.py:146
  73.3 17.6 %collective-permute-start.11 = (bf16[5,72,576]{2,1,0:T(8,128)(2,1)S(1)}, bf16[5,72,576]{2,1,0:T(8,128)(2,1)S(1)}, u32[]{:S(2)}, u32[]{:S(2)}) collective-permute-start(bf16[5,72,576]{2,1,0:T(8,128)(2,1)S(1)} %collective-permute-done.9), channel_id=1, source_target_pairs={{0,30},{2,0},{4,2},{6,4},{8,6},{10,8},{12,10},{14,12},{16,14},{18,... | collective-permute-start | bytes 1244168 | tf_op jit(solution)/shard_map/ppermute | solution.py:151
  78.2 17.7 %collective-permute-start.12 = (bf16[5,72,576]{2,1,0:T(8,128)(2,1)S(1)}, bf16[5,72,576]{2,1,0:T(8,128)(2,1)S(1)}, u32[]{:S(2)}, u32[]{:S(2)}) collective-permute-start(bf16[5,72,576]{2,1,0:T(8,128)(2,1)S(1)} %collective-permute-done.10), channel_id=1, source_target_pairs={{0,2},{2,4},{4,6},{6,8},{8,10},{10,12},{12,14},{14,16},{16,18},{18... | collective-permute-start | bytes 1244168 | tf_op jit(solution)/shard_map/ppermute | solution.py:146
  90.9 14.0 %collective-permute-start.13 = (bf16[5,72,576]{2,1,0:T(8,128)(2,1)S(1)}, bf16[5,72,576]{2,1,0:T(8,128)(2,1)}, u32[]{:S(2)}, u32[]{:S(2)}) collective-permute-start(bf16[5,72,576]{2,1,0:T(8,128)(2,1)S(1)} %collective-permute-done.11), channel_id=1, source_target_pairs={{0,30},{2,0},{4,2},{6,4},{8,6},{10,8},{12,10},{14,12},{16,14},{18,... | collective-permute-start | bytes 1244168 | tf_op jit(solution)/shard_map/ppermute | solution.py:151
  95.9 13.9 %collective-permute-start.14 = (bf16[5,72,576]{2,1,0:T(8,128)(2,1)S(1)}, bf16[5,72,576]{2,1,0:T(8,128)(2,1)}, u32[]{:S(2)}, u32[]{:S(2)}) collective-permute-start(bf16[5,72,576]{2,1,0:T(8,128)(2,1)S(1)} %collective-permute-done.12), channel_id=1, source_target_pairs={{0,2},{2,4},{4,6},{6,8},{8,10},{10,12},{12,14},{14,16},{16,18},{18... | collective-permute-start | bytes 1244168 | tf_op jit(solution)/shard_map/ppermute | solution.py:146
  104.9 46.0 %collective-permute-start.15 = (bf16[5,72,576]{2,1,0:T(8,128)(2,1)}, bf16[5,72,576]{2,1,0:T(8,128)(2,1)}, u32[]{:S(2)}, u32[]{:S(2)}) collective-permute-start(bf16[5,72,576]{2,1,0:T(8,128)(2,1)} %collective-permute-done.13), channel_id=1, source_target_pairs={{0,30},{2,0},{4,2},{6,4},{8,6},{10,8},{12,10},{14,12},{16,14},{18,... | collective-permute-start | bytes 1244168 | tf_op jit(solution)/shard_map/ppermute | solution.py:151
  109.8 41.2 %collective-permute-start.16 = (bf16[5,72,576]{2,1,0:T(8,128)(2,1)}, bf16[5,72,576]{2,1,0:T(8,128)(2,1)S(1)}, u32[]{:S(2)}, u32[]{:S(2)}) collective-permute-start(bf16[5,72,576]{2,1,0:T(8,128)(2,1)} %collective-permute-done.14), channel_id=1, source_target_pairs={{0,2},{2,4},{4,6},{6,8},{8,10},{10,12},{12,14},{14,16},{16,18},{18... | collective-permute-start | bytes 1244168 | tf_op jit(solution)/shard_map/ppermute | solution.py:146
  116.6 16.6 %collective-permute-start = (s32[]{:T(128)}, s32[]{:T(128)}, u32[]{:S(2)}, u32[]{:S(2)}) collective-permute-start(s32[]{:T(128)} %bitcast), channel_id=1, source_target_pairs={{0,1},{1,0},{2,3},{3,2},{4,5},{5,4},{6,7},{7,6},{8,9},{9,8},{10,11... | collective-permute-start | bytes 20 | tf_op jit(solution)/shard_map/ppermute | solution.py:93
  133.8 6.0 collective-permute-start.1
  150.9 184.2 %collective-permute-start.17 = (bf16[5,72,576]{2,1,0:T(8,128)(2,1)}, bf16[5,72,576]{2,1,0:T(8,128)(2,1)}, u32[]{:S(2)}, u32[]{:S(2)}) collective-permute-start(bf16[5,72,576]{2,1,0:T(8,128)(2,1)} %collective-permute-done.15), channel_id=1, source_target_pairs={{0,30},{2,0},{4,2},{6,4},{8,6},{10,8},{12,10},{14,12},{16,14},{18,... | collective-permute-start | bytes 1244168 | tf_op jit(solution)/shard_map/ppermute | solution.py:151
  150.9 199.1 %collective-permute-start.18 = (bf16[5,72,576]{2,1,0:T(8,128)(2,1)S(1)}, bf16[5,72,576]{2,1,0:T(8,128)(2,1)}, u32[]{:S(2)}, u32[]{:S(2)}) collective-permute-start(bf16[5,72,576]{2,1,0:T(8,128)(2,1)S(1)} %collective-permute-done.16), channel_id=1, source_target_pairs={{0,2},{2,4},{4,6},{6,8},{8,10},{10,12},{12,14},{14,16},{16,18},{18... | collective-permute-start | bytes 1244168 | tf_op jit(solution)/shard_map/ppermute | solution.py:146
  368.5 20.5 %collective-permute-start.19 = (bf16[368,1152]{1,0:T(8,128)(2,1)S(1)}, bf16[368,1152]{1,0:T(8,128)(2,1)S(1)}, u32[]{:S(2)}, u32[]{:S(2)}) collective-permute-start(bf16[368,1152]{1,0:T(8,128)(2,1)S(1)} %fusion.27), channel_id=1, source_target_pairs={{0,1},{1,0},{2,3},{3,2},{4,5},{5,4},{6,7},{7,6},{8,9},{9,8},{10,11... | collective-permute-start | bytes 2543624 | tf_op jit(solution)/shard_map/ppermute | solution.py:46
  395.1 13.1 %collective-permute-start.21 = (bf16[2,8,368,72]{2,3,0,1:T(8,128)(2,1)S(1)}, bf16[2,8,368,72]{2,3,0,1:T(8,128)(2,1)S(1)}, u32[]{:S(2)}, u32[]{:S(2)}) collective-permute-start(bf16[2,8,368,72]{2,3,0,1:T(8,128)(2,1)S(1)} %get-tuple-element.50), channel_id=1, source_target_pairs={{0,2},{2,0},{1,3},{3,1},{4,6},{6,4},{5,7},{7,5},{8,10},{10,8},{9,1... | collective-permute-start | bytes 2543624 | tf_op jit(solution)/shard_map/ppermute | solution.py:46
  419.1 21.0 %collective-permute-start.22 = (bf16[368,1152]{1,0:T(8,128)(2,1)S(1)}, bf16[368,1152]{1,0:T(8,128)(2,1)S(1)}, u32[]{:S(2)}, u32[]{:S(2)}) collective-permute-start(bf16[368,1152]{1,0:T(8,128)(2,1)S(1)} %fusion.71), channel_id=1, source_target_pairs={{0,1},{1,0},{2,3},{3,2},{4,5},{5,4},{6,7},{7,6},{8,9},{9,8},{10,11... | collective-permute-start | bytes 2543624 | tf_op jit(solution)/shard_map/ppermute | solution.py:46
  441.2 20.1 %collective-permute-start.23 = (bf16[368,1152]{1,0:T(8,128)(2,1)S(1)}, bf16[368,1152]{1,0:T(8,128)(2,1)S(1)}, u32[]{:S(2)}, u32[]{:S(2)}) collective-permute-start(bf16[368,1152]{1,0:T(8,128)(2,1)S(1)} %add_convert_fusion.1), channel_id=1, source_target_pairs={{0,1},{1,0},{2,3},{3,2},{4,5},{5,4},{6,7},{7,6},{8,9},{9,8},{10,11... | collective-permute-start | bytes 2543624 | tf_op jit(solution)/shard_map/ppermute | solution.py:46
  478.9 19.5 %collective-permute-start.24 = (bf16[368,1152]{1,0:T(8,128)(2,1)}, bf16[368,1152]{1,0:T(8,128)(2,1)}, u32[]{:S(2)}, u32[]{:S(2)}) collective-permute-start(bf16[368,1152]{1,0:T(8,128)(2,1)} %slice.279), channel_id=1, source_target_pairs={{0,1},{1,0},{2,3},{3,2},{4,5},{5,4},{6,7},{7,6},{8,9},{9,8},{10,11... | collective-permute-start | bytes 2543624 | tf_op jit(solution)/shard_map/ppermute | solution.py:46
  502.3 18.4 %collective-permute-start.25 = (bf16[368,1152]{1,0:T(8,128)(2,1)S(1)}, bf16[368,1152]{1,0:T(8,128)(2,1)S(1)}, u32[]{:S(2)}, u32[]{:S(2)}) collective-permute-start(bf16[368,1152]{1,0:T(8,128)(2,1)S(1)} %multiply_convert_fusion.3), channel_id=1, source_target_pairs={{0,1},{1,0},{2,3},{3,2},{4,5},{5,4},{6,7},{7,6},{8,9},{9,8},{10,11... | collective-permute-start | bytes 2543624 | tf_op jit(solution)/shard_map/ppermute | solution.py:46
  548.1 17.8 %collective-permute-start.26 = (bf16[368,1152]{1,0:T(8,128)(2,1)}, bf16[368,1152]{1,0:T(8,128)(2,1)}, u32[]{:S(2)}, u32[]{:S(2)}) collective-permute-start(bf16[368,1152]{1,0:T(8,128)(2,1)} %slice.278), channel_id=1, source_target_pairs={{0,1},{1,0},{2,3},{3,2},{4,5},{5,4},{6,7},{7,6},{8,9},{9,8},{10,11... | collective-permute-start | bytes 2543624 | tf_op jit(solution)/shard_map/ppermute | solution.py:46
  572.7 16.7 %collective-permute-start.27 = (bf16[368,1152]{1,0:T(8,128)(2,1)S(1)}, bf16[368,1152]{1,0:T(8,128)(2,1)S(1)}, u32[]{:S(2)}, u32[]{:S(2)}) collective-permute-start(bf16[368,1152]{1,0:T(8,128)(2,1)S(1)} %convert_element_type.165), channel_id=1, source_target_pairs={{0,1},{1,0},{2,3},{3,2},{4,5},{5,4},{6,7},{7,6},{8,9},{9,8},{10,11... | collective-permute-start | bytes 2543624 | tf_op jit(solution)/shard_map/ppermute | solution.py:46
  602.2 47.1 %collective-permute-start.29 = (bf16[2,8,368,72]{2,3,1,0:T(8,128)(2,1)}, bf16[2,8,368,72]{2,3,1,0:T(8,128)(2,1)}, u32[]{:S(2)}, u32[]{:S(2)}) collective-permute-start(bf16[2,8,368,72]{2,3,1,0:T(8,128)(2,1)} %slice.276), channel_id=1, source_target_pairs={{0,2},{2,0},{1,3},{3,1},{4,6},{6,4},{5,7},{7,5},{8,10},{10,8},{9,1... | collective-permute-start | bytes 2543624 | tf_op jit(solution)/shard_map/ppermute | solution.py:46
  640.3 11.3 %collective-permute-start.28 = (bf16[2,8,368,72]{2,3,1,0:T(8,128)(2,1)S(1)}, bf16[2,8,368,72]{2,3,1,0:T(8,128)(2,1)S(1)}, u32[]{:S(2)}, u32[]{:S(2)}) collective-permute-start(bf16[2,8,368,72]{2,3,1,0:T(8,128)(2,1)S(1)} %slice.277), channel_id=1, source_target_pairs={{0,2},{2,0},{1,3},{3,1},{4,6},{6,4},{5,7},{7,5},{8,10},{10,8},{9,1... | collective-permute-start | bytes 2543624 | tf_op jit(solution)/shard_map/ppermute | solution.py:46
  669.0 200.2 %reduce-scatter.5.cloned.1.call-start = ((), (), s32[]{:S(2)}) async-start(), calls=%async_computation.3 | async-start | bytes 10653696 | tf_op jit(solution)/shard_map/reduce_scatter | solution.py:223
  679.5 20.9 %collective-permute-start.30 = (bf16[368,1152]{1,0:T(8,128)(2,1)}, bf16[368,1152]{1,0:T(8,128)(2,1)S(1)}, u32[]{:S(2)}, u32[]{:S(2)}) collective-permute-start(bf16[368,1152]{1,0:T(8,128)(2,1)} %fusion.72), channel_id=1, source_target_pairs={{0,1},{1,0},{2,3},{3,2},{4,5},{5,4},{6,7},{7,6},{8,9},{9,8},{10,11... | collective-permute-start | bytes 2543624 | tf_op jit(solution)/shard_map/ppermute | solution.py:46
  715.9 13.8 %collective-permute-start.34 = (f32[6913]{0:T(1024)S(1)}, f32[6913]{0:T(1024)S(1)}, u32[]{:S(2)}, u32[]{:S(2)}) collective-permute-start(f32[6913]{0:T(1024)S(1)} %add.445), channel_id=1, source_target_pairs={{0,16},{4,20},{8,24},{12,28},{16,0},{20,4},{24,8},{28,12},{1,17},{... | collective-permute-start | bytes 82964 | tf_op jit(solution)/shard_map/ppermute | solution.py:93
  (80 other events, 1540.7 us)
Sparse Core Ops, SparseCore 0:
  10.8 120.2 all-gather.1
  669.1 82.9 reduce-scatter.6
  756.2 112.9 reduce-scatter.4
